TPU v7x, 32 devices: a whole 2x2x4 slice. The times are simulated.
32 devices in a mesh: gz: 4 (over x, core), gx: 4 (over z), gy: 2 (over y).
Axes of the slice: x: 2, y: 2, z: 4, core: 2. Of those that a mesh axis runs over, the one named last changes fastest.
Arguments:
- offsets: float32 [3, 4, 8, 8, 128], P(None, 'gz', 'gx', 'gy'), may hold values from 0 to 10
- type_ids: int32 [4, 8, 8, 128], P('gz', 'gx', 'gy'), may hold values from 0 to 2
- occupied: int32 [4, 8, 8, 128], P('gz', 'gx', 'gy'), may hold values from 0 to 1, as said below
- prior_charges: float32 [2, 4, 8, 8, 128], P(None, 'gz', 'gx', 'gy'), may hold values from -0.6 to 0.6
- electronegativity: float32 [3], replicated, may hold values from 2 to 10
- hardness: float32 [3], replicated, may hold values from 4 to 12
- shielding: float32 [3], replicated, may hold values from 0.5 to 1.2
Outputs:
- charges: float32 [4, 8, 8, 128], P('gz', 'gx', 'gy')
- residuals: float32 [2, 4, 8, 8, 128], P(None, 'gz', 'gx', 'gy')
Inputs may be any that keep to these rules, and one draw needn't show every extreme that they name: `occupied`: 1 marks a slot that holds an atom, 0 a padding slot.
All inputs are finite; a program needn't handle non-finite values.
Results may differ from a plain program's by a relative error of at most 0.00021.
Values sent between devices are 32-bit elements; how exact they have to be, the bound alone decides.
A program may use at most 128 MiB of HBM per device.

v0:
```python
import functools

import jax
import jax.numpy as jnp
from jax import lax
from jax.experimental import pallas as pl
from jax.experimental.pallas import tpu as pltpu
from jax.sharding import PartitionSpec as P

ITERS = 4
AXES = ("gz", "gx", "gy")
MESH = pl.DeviceIdType.MESH

coulomb_factor = 14.4
cell_edge = 10.0
CHUNK = 64


def kernel(
    sizes, dys,
    offsets_in, type_ids_in, occupied_in, prior_in, electro_in, hardness_in, shielding_in,
    charges, residuals,
    offsets, type_ids, occupied, prior, electro, hardness, shielding,
    first, fields, first_edge, edges, pair, local, sums, parts, mine,
    in_sem, send_sem, recv_sem, part_send, part_recv,
):
    loads = [
        pltpu.make_async_copy(source, target, in_sem.at[k])
        for k, (source, target) in enumerate(
            zip(
                (offsets_in, type_ids_in, occupied_in, prior_in,
                 electro_in, hardness_in, shielding_in),
                (offsets, type_ids, occupied, prior, electro, hardness, shielding),
            )
        )
    ]
    for load in loads:
        load.start()
    nz, nx, ny = sizes
    cells_x, cells_y, slots = type_ids.shape[1:]
    rows = 2 * cells_y
    geo_rows = 4 * cells_y
    cells = cells_x * cells_y
    devices = nz * nx * ny
    sides = len(dys) - 1
    me_z, me_x, me_y = (lax.axis_index(name) for name in AXES)

    at_x = [lax.rem(me_x + d, nx) for d in range(nx)]
    at_y = [lax.rem(me_y + d, ny) for d in range(ny)]

    def each_peer(action):
        def layer(dz, skip):
            z = lax.rem(me_z + dz, nz)
            for dx in range(nx):
                for dy in range(ny):
                    if not (skip and dx == 0 and dy == 0):
                        action((z, at_x[dx], at_y[dy]), (dz * nx + dx) * ny + dy - 1)

        layer(0, True)
        if nz <= 4:
            for dz in range(1, nz):
                layer(dz, False)
        else:
            pl.loop(1, nz)(lambda dz: layer(dz, False))

    barrier = pltpu.get_barrier_semaphore()
    each_peer(
        lambda peer, slot: pl.semaphore_signal(
            barrier, inc=1, device_id=peer, device_id_type=MESH
        )
    )

    def per_atom(table, ids):
        summed = jnp.zeros(ids.shape, jnp.float32)
        for species in range(table.shape[0]):
            summed = summed + jnp.where(ids == species, table[species], 0.0)
        return summed

    for load in loads:
        load.wait()
    occ, stiff, rhs, x = [], [], [], []

    def ends(values):
        return [values[:1], values[cells_y - 1 : cells_y]]

    for i in range(cells_x):
        ids = type_ids[0, i]
        occ_i = occupied[0, i].astype(jnp.float32)
        radius = per_atom(shielding, ids) * (1.0 / cell_edge)
        geo = [offsets[c, 0, i] * (1.0 / cell_edge) for c in range(3)] + [radius * radius]
        first[1, i + 1, :geo_rows] = jnp.concatenate(geo, axis=0)
        stiff_i = per_atom(hardness, ids)
        affinity = per_atom(electro, ids)
        occ.append(jnp.concatenate([occ_i, occ_i], axis=0))
        stiff.append(jnp.concatenate([stiff_i, stiff_i], axis=0))
        rhs.append(jnp.concatenate([-affinity * occ_i, -occ_i], axis=0))
        start = jnp.concatenate([prior[0, 0, i] * occ_i, prior[1, 0, i] * occ_i], axis=0)
        x.append(start)
        first[1, i + 1, geo_rows : geo_rows + rows] = start
        pieces = geo + [start[:cells_y], start[cells_y:]]
        first_edge[i] = jnp.concatenate([end for v in pieces for end in ends(v)], axis=0)

    for edge, slot in ((0, 0), (nz - 1, 2)):

        @pl.when(me_z == edge)
        def _():
            first[slot] = jnp.zeros(first.shape[1:], jnp.float32)
            for k in range(ITERS):
                fields[k, slot] = jnp.zeros(fields.shape[2:], jnp.float32)

    messages = [
        (dz, dx, dy)
        for dz in (1, -1, 0)
        for dx in (1, -1, 0)
        for dy in reversed(dys)
        if (dz, dx, dy) != (0, 0, 0)
    ]
    turn_x = {d: lax.rem(me_x + d + nx, nx) for d in (0, 1, -1)}
    turn_y = {d: lax.rem(me_y + d + ny, ny) for d in (0, 1, -1)}

    def copies(stage, buffer, edge, own_rows, action, layers=(1, -1, 0)):
        edge_rows = edge.shape[1]
        for m, (dz, dx, dy) in enumerate(messages):
            if dz not in layers:
                continue
            source, target, count = {
                0: (0, 1, cells_x),
                1: (cells_x - 1, 0, 1),
                -1: (0, cells_x + 1, 1),
            }[dx]
            if dy == 0:
                src = buffer.at[1, pl.ds(source + 1, count), pl.ds(0, own_rows)]
                span = pl.ds(0, own_rows)
            else:
                src = edge.at[pl.ds(source, count)]
                span = pl.ds(own_rows + (dys.index(dy) - 1) * edge_rows, edge_rows)
            copy = pltpu.make_async_remote_copy(
                src_ref=src,
                dst_ref=buffer.at[1 - dz, pl.ds(target, count), span],
                send_sem=send_sem.at[stage, m],
                recv_sem=recv_sem.at[stage, m],
                device_id=(me_z + dz, turn_x[dx], turn_y[dy]),
                device_id_type=MESH,
            )
            action(copy, dz)

    def guarded(name, sign):
        def go(copy, dz):
            act = getattr(copy, name)
            if dz == 0:
                act()
            else:
                other = me_z + sign * dz
                pl.when((other >= 0) & (other < nz))(act)

        return go

    def send(*what):
        copies(*what, guarded("start", 1))

    def receive(*what, layers=(1, -1, 0)):
        copies(*what, guarded("wait_recv", -1), layers)

    def sent(*what):
        copies(*what, guarded("wait_send", 1))

    opening = (0, first, first_edge, geo_rows + rows)
    pl.semaphore_wait(barrier, devices - 1)
    send(*opening)

    shape = (slots, slots)
    eye = lax.broadcasted_iota(jnp.int32, shape, 0) == lax.broadcasted_iota(jnp.int32, shape, 1)

    @pl.loop(0, cells)
    def _(cell):
        i, j = cell // cells_y, cell % cells_y
        for c in range(4):
            row = first[1, i + 1, pl.ds(c * cells_y + j, 1), :]
            column = jnp.sum(jnp.where(eye, row, 0.0), axis=1, keepdims=True)
            local[cell, c] = jnp.broadcast_to(column, shape)

    def row_at(q, y, base, own_rows, edge_base, edge_rows):
        if y < 0:
            return own_rows + edge_base + 2 * q + 1
        if y >= cells_y:
            return own_rows + (sides - 1) * edge_rows + edge_base + 2 * q
        return base + q * cells_y + y

    geo_rule = (0, geo_rows + rows, 0, 12)
    start_rule = (geo_rows, geo_rows + rows, 8, 12)
    field_rule = (0, rows, 0, 4)

    def inside(i):
        return [1, 2 - 2 * i] if cells_x == 2 else [1]

    def outside(i):
        return [2 * i] if cells_x == 2 else [0, 2]

    def in_block(j, k):
        return 0 <= j + k - 1 < cells_y

    def couple(i, j, dz, dx, k):
        cell = i * cells_y + j
        tile = first.at[dz, i + dx]

        def line(q):
            at = row_at(q, j + k - 1, *geo_rule)
            return tile[at : at + 1, :]

        bz = line(0) + (jnp.asarray(dz, jnp.int32) - 1).astype(jnp.float32)
        bx = line(1) + (jnp.asarray(dx, jnp.int32) - 1).astype(jnp.float32)
        by = line(2) + (k - 1.0)
        bs = line(3)
        for part in range(slots // CHUNK):
            span = pl.ds(part * CHUNK, CHUNK)
            ez = bz - local[cell, 0, span]
            ex = bx - local[cell, 1, span]
            ey = by - local[cell, 2, span]
            squared = ez * ez + ex * ex + ey * ey
            fraction = squared * lax.rsqrt(jnp.maximum(squared, 1e-30))
            reach = jnp.maximum(1.0 - fraction, 0.0)
            reach = reach * reach
            factor = coulomb_factor / cell_edge
            taper = reach * reach * (4.0 * factor * fraction + factor)
            pair[cell, (dz * 3 + dx) * 3 + k, span] = taper * lax.rsqrt(
                squared + (local[cell, 3, span] + bs)
            )

    def build():
        @pl.loop(0, cells_x)
        def _(i):
            for dx in inside(i):
                for j in range(cells_y):
                    for k in range(3):
                        if in_block(j, k):
                            couple(i, j, 1, dx, k)

        receive(*opening, layers=(0,))

        @pl.loop(0, cells_x)
        def _(i):
            for dx in outside(i):
                for j in range(cells_y):
                    for k in range(3):
                        couple(i, j, 1, dx, k)
            for dx in inside(i):
                for j in range(cells_y):
                    for k in range(3):
                        if not in_block(j, k):
                            couple(i, j, 1, dx, k)

        receive(*opening, layers=(1, -1))

        @pl.loop(0, cells_x)
        def _(i):
            @pl.loop(0, 6)
            def _(plane):
                dz, dx = 2 * (plane // 3), plane % 3
                for j in range(cells_y):
                    for k in range(3):
                        couple(i, j, dz, dx, k)

    def add_pairs(buffer, rule, i, j, total, planes, chosen):
        for dz, dx in planes:
            for k in range(3):
                if not chosen(dz, dx, k):
                    continue
                tile = buffer.at[dz, i + dx]
                block = pair[i * cells_y + j, (dz * 3 + dx) * 3 + k]
                for s in range(2):
                    at = row_at(s, j + k - 1, *rule)
                    total[s] = total[s] + block * tile[at : at + 1, :]
        return total

    def operate_own(buffer, rule):
        @pl.loop(0, cells_x)
        def _(i):
            for j in range(cells_y):
                total = [jnp.zeros(shape, jnp.float32) for _ in range(2)]
                total = add_pairs(
                    buffer, rule, i, j, total,
                    [(1, dx) for dx in inside(i)], lambda dz, dx, k: in_block(j, k),
                )
                for s in range(2):
                    sums[i, s * cells_y + j] = total[s]

    def accumulate(buffer, rule, groups):
        @pl.loop(0, cells_x)
        def _(i):
            for j in range(cells_y):
                total = [sums[i, s * cells_y + j] for s in range(2)]
                for planes, chosen in groups(i, j):
                    total = add_pairs(buffer, rule, i, j, total, planes, chosen)
                for s in range(2):
                    sums[i, s * cells_y + j] = total[s]

    even = lax.rem(me_z, 2) == 0
    near = jnp.where(even, 2, 0)
    far = 2 - near

    def all_pairs(dz, dx, k):
        return True

    def operate_rest(buffer, rule, field, arrived=None):
        if arrived is not None:
            arrived(0)
        accumulate(
            buffer, rule,
            lambda i, j: [
                ([(1, dx) for dx in inside(i)], lambda dz, dx, k: not in_block(j, k)),
                ([(1, dx) for dx in outside(i)], all_pairs),
                ([(near, dx) for dx in range(3)], all_pairs),
            ],
        )
        if arrived is not None:
            arrived(1)
        accumulate(
            buffer, rule, lambda i, j: [([(far, dx) for dx in range(3)], all_pairs)]
        )

        out = []
        for i in range(cells_x):
            lines = []
            for row in range(rows):
                column = jnp.sum(sums[i, row], axis=1, keepdims=True)
                lines.append(jnp.sum(jnp.where(eye, column, 0.0), axis=0, keepdims=True))
            out.append(occ[i] * (stiff[i] * field[i] + jnp.concatenate(lines, axis=0)))
        return out

    tile_shape = (rows, slots)
    lane = lax.broadcasted_iota(jnp.int32, tile_shape, 1)
    second = lax.broadcasted_iota(jnp.int32, tile_shape, 0) >= cells_y
    slot_of = lane - jnp.where(second, 8, 0)

    def part_copy(stage, peer, slot):
        return pltpu.make_async_remote_copy(
            src_ref=mine.at[stage],
            dst_ref=parts.at[stage, slot],
            send_sem=part_send.at[stage],
            recv_sem=part_recv.at[stage],
            device_id=peer,
            device_id_type=MESH,
        )

    def start_sums(stage, quantities):
        packed = jnp.zeros(tile_shape, jnp.float32)
        for k, quantity in enumerate(quantities):
            column = jnp.sum(functools.reduce(jnp.add, quantity), axis=1, keepdims=True)
            packed = jnp.where(slot_of == k, column, packed)
        mine[stage] = jnp.sum(packed, axis=0, keepdims=True)
        each_peer(lambda peer, slot: part_copy(stage, peer, slot).start())

    def finish_sums(stage, count):
        everything = parts.at[stage]
        pltpu.make_async_copy(everything, everything, part_recv.at[stage]).wait()
        row = mine[stage] + jnp.sum(parts[stage], axis=0)
        pltpu.make_async_copy(everything, everything, part_send.at[stage]).wait()
        return [
            jnp.where(
                second,
                jnp.broadcast_to(row[:, 8 + k : 9 + k], tile_shape),
                jnp.broadcast_to(row[:, k : k + 1], tile_shape),
            )
            for k in range(count)
        ]

    span = range(cells_x)

    def exchange_and_operate(stage, field, meanwhile=None):
        buffer, edge = fields.at[stage - 1], edges.at[stage - 1]
        for i in span:
            buffer[1, i + 1, :rows] = field[i]
            pieces = [field[i][:cells_y], field[i][cells_y:]]
            edge[i] = jnp.concatenate([end for v in pieces for end in ends(v)], axis=0)
        what = (stage, buffer, edge, rows)
        send(*what)
        if meanwhile is not None:
            meanwhile()
        operate_own(buffer, field_rule)


        def arrived(step):
            for layer in (1, -1):
                now = (near if step == 0 else far) == 1 - layer
                pl.when(now)(lambda: receive(*what, layers=(layer,)))
            if step == 0:
                receive(*what, layers=(0,))

        out = operate_rest(buffer, field_rule, field, arrived)
        sent(*what)
        return out

    build()
    operate_own(first, start_rule)
    image = operate_rest(first, start_rule, x)
    sent(*opening)
    r = [rhs[i] - image[i] for i in span]
    w = exchange_and_operate(1, r)

    p = s = z = None
    for stage in range(ITERS):
        quantities = [[r[i] * r[i] for i in span], [w[i] * r[i] for i in span]]
        last = stage == ITERS - 1
        if last:
            quantities += [x, r, p]
        go = functools.partial(start_sums, stage, quantities)
        n = go() if last else exchange_and_operate(stage + 2, w, go)
        found = finish_sums(stage, len(quantities))
        gamma, delta = found[:2]
        if stage == 0:
            beta = None
            alpha = gamma / delta
            p, s, z = r, w, n
        else:
            beta = gamma / gamma_before
            alpha = gamma / (delta - beta * gamma / alpha)
            p = [r[i] + beta * p[i] for i in span]
            s = [w[i] + beta * s[i] for i in span]
            if not last:
                z = [n[i] + beta * z[i] for i in span]
        gamma_before = gamma
        x = [x[i] + alpha * p[i] for i in span]
        r = [r[i] - alpha * s[i] for i in span]
        if not last:
            w = [w[i] - alpha * z[i] for i in span]
    totals = found[2] + alpha * (found[3] + beta * found[4])
    ratio = totals[:cells_y] / totals[cells_y:]
    for i in span:
        charges[0, i] = x[i][:cells_y] - ratio * x[i][cells_y:]
        residuals[0, 0, i] = r[i][:cells_y]
        residuals[1, 0, i] = r[i][cells_y:]


def per_device(sizes, *arrays):
    type_ids = arrays[1]
    cells_x, cells_y, slots = type_ids.shape[1:]
    cells = cells_x * cells_y
    rows = 2 * cells_y
    devices = sizes[0] * sizes[1] * sizes[2]
    dys = (0, 1) if sizes[2] == 2 else (0, 1, -1)
    messages = 9 * len(dys) - 1
    halo = (3, cells_x + 2)
    sides = len(dys) - 1
    vmem = pl.BlockSpec(memory_space=pltpu.VMEM)
    return pl.pallas_call(
        functools.partial(kernel, sizes, dys),
        out_shape=(
            jax.ShapeDtypeStruct(type_ids.shape, jnp.float32),
            jax.ShapeDtypeStruct((2,) + type_ids.shape, jnp.float32),
        ),
        in_specs=[pl.BlockSpec(memory_space=pl.ANY)] * 7,
        out_specs=(vmem, vmem),
        scratch_shapes=[
            *(pltpu.VMEM(array.shape, array.dtype) for array in arrays[:4]),
            *(pltpu.SMEM(array.shape, array.dtype) for array in arrays[4:]),
            pltpu.VMEM(halo + (6 * cells_y + 12 * sides, slots), jnp.float32),
            pltpu.VMEM((ITERS,) + halo + (rows + 4 * sides, slots), jnp.float32),
            pltpu.VMEM((cells_x, 12, slots), jnp.float32),
            pltpu.VMEM((ITERS, cells_x, 4, slots), jnp.float32),
            pltpu.VMEM((cells, 27, slots, slots), jnp.float32),
            pltpu.VMEM((cells, 4, slots, slots), jnp.float32),
            pltpu.VMEM((cells_x, rows, slots, slots), jnp.float32),
            pltpu.VMEM((ITERS, devices - 1, 1, slots), jnp.float32),
            pltpu.VMEM((ITERS, 1, slots), jnp.float32),
            pltpu.SemaphoreType.DMA((len(arrays),)),
            pltpu.SemaphoreType.DMA((ITERS + 1, messages)),
            pltpu.SemaphoreType.DMA((ITERS + 1, messages)),
            pltpu.SemaphoreType.DMA((ITERS,)),
            pltpu.SemaphoreType.DMA((ITERS,)),
        ],
        compiler_params=pltpu.CompilerParams(
            collective_id=0, has_side_effects=True, vmem_limit_bytes=60 * 1024 * 1024
        ),
    )(*arrays)


def solution(mesh):
    sizes = tuple(mesh.shape[name] for name in AXES)
    in_specs = (
        P(None, "gz", "gx", "gy", None),
        P("gz", "gx", "gy", None),
        P("gz", "gx", "gy", None),
        P(None, "gz", "gx", "gy", None),
        P(),
        P(),
        P(),
    )
    out_specs = (P("gz", "gx", "gy", None), P(None, "gz", "gx", "gy", None))
    return jax.shard_map(
        functools.partial(per_device, sizes),
        mesh=mesh,
        in_specs=in_specs,
        out_specs=out_specs,
        check_vma=False,
    )
```

profile of v0, /device:TPU:0, one launch (start us, length us, event | category | flops | bytes accessed | tf_op | source)
XLA Modules:
  0.0 57.4 jit_solution(16229513211070676840)
XLA Ops:
  0.6 54.9 %shard_map.86 = (f32[1,2,4,128]{3,2,1,0:T(4,128)}, f32[2,1,2,4,128]{4,3,2,1,0:T(4,128)}) custom-call(f32[3,1,2,4,128]{4,3,2,1,0:T(4,128)} %offsets_in.1, s32[1,2,4,128]{3,2,1,0:T(4,128)} %type_ids_in.1, s32[1,2,4,128]{3,2,1,0:T(4,128)} %occupied_in.1, f32[2,1,2,4,128]{4,3,2,1,0:T(4,128)} %prior_in.1, f32[3]{0:T(128)} %electro_in.1, f32[3]{0:T(128)} %hardness_in.1, ...), custom_call_target="tpu_custom_call" | custom-call | tf_op jit(solution)/shard_map/pallas_call | solution.py:445
  55.5 0.0 copy-start
  55.5 1.3 %copy.11 = f32[1,2,4,128]{3,2,1,0:T(4,128)} copy(f32[1,2,4,128]{3,2,1,0:T(4,128)} %get-tuple-element.4) | data formatting | bytes 8192
  56.8 0.0 copy-done
  56.8 0.6 %copy.12 = f32[2,1,2,4,128]{4,3,2,1,0:T(4,128)} copy(f32[2,1,2,4,128]{4,3,2,1,0:T(4,128)S(1)} %copy-done) | data formatting | bytes 16384
Async XLA Ops:
  55.5 1.3 %copy-start = (f32[2,1,2,4,128]{4,3,2,1,0:T(4,128)S(1)}, f32[2,1,2,4,128]{4,3,2,1,0:T(4,128)}, u32[]{:S(2)}) copy-start(f32[2,1,2,4,128]{4,3,2,1,0:T(4,128)} %get-tuple-element.5) | copy-start | bytes 24580
where the time goes:
time: 57.6 us; the launch traced here: 57.4 us
  Pallas kernels  54.9 us (95%)
  local copies, waits for them, and re-layouts  1.88 us (3%)
  between operations  0.65 us (1%)
    pallas_call x1, Pallas kernels, per_device(): pl.pallas_call(functools.partial(kernel, sizes, dys), out_shape=(jax.Shap...  54.9 us
    unnamed x4, local copies, waits for them, and re-layouts  1.88 us

commit v1 on v0

--- a/solution.py
+++ b/solution.py
@@ -14,6 +14,9 @@
 coulomb_factor = 14.4
 cell_edge = 10.0
 CHUNK = 64
+EDGE = (4.0 * coulomb_factor / cell_edge) ** 0.25
+SCALE = EDGE / cell_edge
+DEPTH = 64
 
 
 def kernel(
@@ -21,7 +24,7 @@
     offsets_in, type_ids_in, occupied_in, prior_in, electro_in, hardness_in, shielding_in,
     charges, residuals,
     offsets, type_ids, occupied, prior, electro, hardness, shielding,
-    first, fields, first_edge, edges, pair, local, sums, parts, mine,
+    first, fields, first_edge, edges, pair, left, right, sums, image, parts, mine,
     in_sem, send_sem, recv_sem, part_send, part_recv,
 ):
     loads = [
@@ -86,8 +89,8 @@
     for i in range(cells_x):
         ids = type_ids[0, i]
         occ_i = occupied[0, i].astype(jnp.float32)
-        radius = per_atom(shielding, ids) * (1.0 / cell_edge)
-        geo = [offsets[c, 0, i] * (1.0 / cell_edge) for c in range(3)] + [radius * radius]
+        radius = per_atom(shielding, ids) * SCALE
+        geo = [offsets[c, 0, i] * SCALE for c in range(3)] + [radius * radius]
         first[1, i + 1, :geo_rows] = jnp.concatenate(geo, axis=0)
         stiff_i = per_atom(hardness, ids)
         affinity = per_atom(electro, ids)
@@ -110,19 +113,18 @@
 
     messages = [
         (dz, dx, dy)
+        for dx_set, dy_set in (((1, -1), dys[1:]), ((1, -1), (0,)), ((0,), dys[1:]), ((0,), (0,)))
         for dz in (1, -1, 0)
-        for dx in (1, -1, 0)
-        for dy in reversed(dys)
+        for dx in dx_set
+        for dy in dy_set
         if (dz, dx, dy) != (0, 0, 0)
     ]
     turn_x = {d: lax.rem(me_x + d + nx, nx) for d in (0, 1, -1)}
     turn_y = {d: lax.rem(me_y + d + ny, ny) for d in (0, 1, -1)}
 
-    def copies(stage, buffer, edge, own_rows, action, layers=(1, -1, 0)):
+    def each_message(stage, buffer, edge, own_rows, name):
         edge_rows = edge.shape[1]
-        for m, (dz, dx, dy) in enumerate(messages):
-            if dz not in layers:
-                continue
+        for dz, dx, dy in messages:
             source, target, count = {
                 0: (0, 1, cells_x),
                 1: (cells_x - 1, 0, 1),
@@ -134,35 +136,53 @@
             else:
                 src = edge.at[pl.ds(source, count)]
                 span = pl.ds(own_rows + (dys.index(dy) - 1) * edge_rows, edge_rows)
+            at = (stage, 1 - dz, 1 - dx, dys.index(dy))
             copy = pltpu.make_async_remote_copy(
                 src_ref=src,
                 dst_ref=buffer.at[1 - dz, pl.ds(target, count), span],
-                send_sem=send_sem.at[stage, m],
-                recv_sem=recv_sem.at[stage, m],
+                send_sem=send_sem.at[at],
+                recv_sem=recv_sem.at[at],
                 device_id=(me_z + dz, turn_x[dx], turn_y[dy]),
                 device_id_type=MESH,
             )
-            action(copy, dz)
-
-    def guarded(name, sign):
-        def go(copy, dz):
             act = getattr(copy, name)
             if dz == 0:
                 act()
             else:
-                other = me_z + sign * dz
+                other = me_z + dz
                 pl.when((other >= 0) & (other < nz))(act)
 
-        return go
-
     def send(*what):
-        copies(*what, guarded("start", 1))
-
-    def receive(*what, layers=(1, -1, 0)):
-        copies(*what, guarded("wait_recv", -1), layers)
+        each_message(*what, "start")
 
     def sent(*what):
-        copies(*what, guarded("wait_send", 1))
+        each_message(*what, "wait_send")
+
+    def receive(what, plane, side, across):
+        stage, buffer, edge, own_rows = what
+        edge_rows = edge.shape[1]
+        count = cells_x if isinstance(side, int) and side == 1 else 1
+        for d in range(len(dys)):
+            if (d == 0) == across:
+                continue
+            rows_in = edge_rows if across else own_rows
+            landed = buffer.at[1, pl.ds(1, count), pl.ds(0, rows_in)]
+            pltpu.make_async_copy(landed, landed, recv_sem.at[stage, plane, side, d]).wait()
+
+    even = lax.rem(me_z, 2) == 0
+    near = jnp.where(even, 2, 0)
+    far = 2 - near
+    has_far = (me_z + far >= 1) & (me_z + far <= nz)
+    has_near = (me_z + near >= 1) & (me_z + near <= nz)
+    early = jnp.where(me_x == nx - 1, 0, 2)
+
+    def receive_planes(what, planes, side, across):
+        for plane in planes:
+            if isinstance(plane, int):
+                receive(what, plane, side, across)
+            else:
+                there = has_near if plane is near else has_far
+                pl.when(there)(lambda plane=plane: receive(what, plane, side, across))
 
     opening = (0, first, first_edge, geo_rows + rows)
     pl.semaphore_wait(barrier, devices - 1)
@@ -170,14 +190,6 @@
 
     shape = (slots, slots)
     eye = lax.broadcasted_iota(jnp.int32, shape, 0) == lax.broadcasted_iota(jnp.int32, shape, 1)
-
-    @pl.loop(0, cells)
-    def _(cell):
-        i, j = cell // cells_y, cell % cells_y
-        for c in range(4):
-            row = first[1, i + 1, pl.ds(c * cells_y + j, 1), :]
-            column = jnp.sum(jnp.where(eye, row, 0.0), axis=1, keepdims=True)
-            local[cell, c] = jnp.broadcast_to(column, shape)
 
     def row_at(q, y, base, own_rows, edge_base, edge_rows):
         if y < 0:
@@ -193,139 +205,226 @@
     def inside(i):
         return [1, 2 - 2 * i] if cells_x == 2 else [1]
 
-    def outside(i):
-        return [2 * i] if cells_x == 2 else [0, 2]
-
     def in_block(j, k):
         return 0 <= j + k - 1 < cells_y
 
+    group = lax.broadcasted_iota(jnp.int32, (8, slots), 0)
+    role = lax.rem(group, 4)
+    lower = group < 4
+    ones = jnp.where(group < 3, 1.0, 0.0)
+    nought = jnp.zeros((8, slots), jnp.float32)
+
+    def split(values):
+        pieces = []
+        for _ in range(3):
+            piece = values.astype(jnp.bfloat16).astype(jnp.float32)
+            pieces.append(piece)
+            values = values - piece
+        return pieces
+
+    def place(dz, dx, y):
+        start = row_at(0, y, *geo_rule)
+        step = cells_y if 0 <= y < cells_y else 2
+        four = first[dz, dx, pl.ds(start, 4, stride=step), :]
+        both = jnp.concatenate([four, four], axis=0)
+        centre_z = (jnp.asarray(dz, jnp.int32).astype(jnp.float32) - 1.5) * EDGE
+        centre_x = (jnp.asarray(dx, jnp.int32).astype(jnp.float32) - (1.0 + cells_x / 2)) * EDGE
+        centre_y = (y - cells_y / 2) * EDGE
+        moved = both + jnp.where(
+            role == 0, centre_z, jnp.where(role == 1, centre_x, jnp.where(role == 2, centre_y, 0.0))
+        )
+        squares = jnp.where((role == 3) | (group > 3), 0.0, moved * moved)
+        return moved, jnp.sum(squares, axis=0, keepdims=True), four[3:4]
+
+    def slot_at(dz, dx, y):
+        return (dz * (cells_x + 2) + dx) * (cells_y + 2) + y + 1
+
+    def offer(dz, dx, y):
+        moved, length, spread = place(dz, dx, y)
+        last = jnp.where(lower, length, length + spread)
+        p1, p2, p3 = split(jnp.where(role == 3, last, moved))
+        to = slot_at(dz, dx, y)
+        for half in range(2):
+            kept = [
+                jnp.where(lower, p, 0.0) if half == 0 else jnp.where(lower, 0.0, p)
+                for p in (p1, p2, p3)
+            ]
+            lines = [kept[q] for q in (0, 1, 2, 0, 1, 0)] + [ones, ones if half else nought]
+            right[to, :, half * slots : (half + 1) * slots] = jnp.concatenate(
+                lines, axis=0
+            ).astype(jnp.bfloat16)
+
+    def take(i, j):
+        moved, length, spread = place(1, i + 1, j)
+        a1, a2, a3 = split(-2.0 * moved)
+
+        def stacked(value):
+            v1, v2, v3 = split(value)
+            return jnp.where(group == 0, v1, jnp.where(group == 1, v2, jnp.where(group == 2, v3, 0.0)))
+
+        one = jnp.where(role == 3, 1.0, a1)
+        two = jnp.where(role == 3, 0.0, a2)
+        three = jnp.where(role == 3, 0.0, a3)
+        lines = [one, one, one, two, two, three, stacked(length), stacked(spread)]
+        left[i * cells_y + j] = jnp.concatenate(lines, axis=0).T.astype(jnp.bfloat16)
+
     def couple(i, j, dz, dx, k):
         cell = i * cells_y + j
-        tile = first.at[dz, i + dx]
-
-        def line(q):
-            at = row_at(q, j + k - 1, *geo_rule)
-            return tile[at : at + 1, :]
-
-        bz = line(0) + (jnp.asarray(dz, jnp.int32) - 1).astype(jnp.float32)
-        bx = line(1) + (jnp.asarray(dx, jnp.int32) - 1).astype(jnp.float32)
-        by = line(2) + (k - 1.0)
-        bs = line(3)
+        other = right[slot_at(dz, i + dx, j + k - 1)]
         for part in range(slots // CHUNK):
             span = pl.ds(part * CHUNK, CHUNK)
-            ez = bz - local[cell, 0, span]
-            ex = bx - local[cell, 1, span]
-            ey = by - local[cell, 2, span]
-            squared = ez * ez + ex * ex + ey * ey
-            fraction = squared * lax.rsqrt(jnp.maximum(squared, 1e-30))
-            reach = jnp.maximum(1.0 - fraction, 0.0)
+            both = jnp.dot(left[cell, span], other, preferred_element_type=jnp.float32)
+            squared = jnp.maximum(both[:, :slots], 1e-30)
+            apart = squared * lax.rsqrt(squared)
+            reach = jnp.maximum(EDGE - apart, 0.0)
             reach = reach * reach
-            factor = coulomb_factor / cell_edge
-            taper = reach * reach * (4.0 * factor * fraction + factor)
-            pair[cell, (dz * 3 + dx) * 3 + k, span] = taper * lax.rsqrt(
-                squared + (local[cell, 3, span] + bs)
+            pair[cell, (dz * 3 + dx) * 3 + k, span] = (
+                reach * reach * (apart + EDGE / 4) * lax.rsqrt(both[:, slots:])
             )
 
-    def build():
+    ends_y = sorted({0, cells_y - 1})
+
+    def build(what):
+        def plane(dz):
+            @pl.loop(0, cells_x)
+            def _(i):
+                for y in range(cells_y):
+                    offer(dz, i + 1, y)
+
+            @pl.loop(0, cells_x)
+            def _(i):
+                for j in range(cells_y):
+                    for dx in inside(i):
+                        for k in range(3):
+                            if in_block(j, k):
+                                couple(i, j, dz, dx, k)
+
         @pl.loop(0, cells_x)
         def _(i):
-            for dx in inside(i):
+            for j in range(cells_y):
+                take(i, j)
+
+        plane(1)
+        for dz in (near, far):
+            receive_planes(what, (dz,), 1, False)
+            plane(dz)
+        receive_planes(what, (1, near, far), 1, True)
+        for dz in (1, near, far):
+
+            @pl.loop(0, cells_x)
+            def _(i):
+                for y in (-1, cells_y):
+                    offer(dz, i + 1, y)
+
+        @pl.loop(0, cells_x)
+        def _(i):
+            for dz in (1, near, far):
+                for j in ends_y:
+                    for dx in inside(i):
+                        for k in range(3):
+                            if not in_block(j, k):
+                                couple(i, j, dz, dx, k)
+
+        @pl.loop(0, 2)
+        def _(turn):
+            side = jnp.where(turn == 0, early, 2 - early)
+            i = (cells_x - 1) * (side // 2)
+            receive_planes(what, (1, near, far), side, False)
+            for dz in (1, near, far):
+                for y in range(cells_y):
+                    offer(dz, i + side, y)
+            for dz in (1, near, far):
                 for j in range(cells_y):
                     for k in range(3):
                         if in_block(j, k):
-                            couple(i, j, 1, dx, k)
-
-        receive(*opening, layers=(0,))
+                            couple(i, j, dz, side, k)
+            receive_planes(what, (1, near, far), side, True)
+            for dz in (1, near, far):
+                for y in (-1, cells_y):
+                    offer(dz, i + side, y)
+            for dz in (1, near, far):
+                for j in ends_y:
+                    for k in range(3):
+                        if not in_block(j, k):
+                            couple(i, j, dz, side, k)
+
+    def add_pairs(buffer, rule, i, j, entries, fresh):
+        if fresh:
+            total = [jnp.zeros(shape, jnp.float32) for _ in range(2)]
+        else:
+            total = [sums[i, s * cells_y + j] for s in range(2)]
+        for dz, dx, k in entries:
+            tile = buffer.at[dz, i + dx]
+            block = pair[i * cells_y + j, (dz * 3 + dx) * 3 + k]
+            for s in range(2):
+                at = row_at(s, j + k - 1, *rule)
+                total[s] = total[s] + block * tile[at : at + 1, :]
+        for s in range(2):
+            sums[i, s * cells_y + j] = total[s]
+
+    def gather(i):
+        lines = []
+        for row in range(rows):
+            column = jnp.sum(sums[i, row], axis=1, keepdims=True)
+            lines.append(jnp.sum(jnp.where(eye, column, 0.0), axis=0, keepdims=True))
+        image[i] = jnp.concatenate(lines, axis=0)
+
+    def operate(buffer, rule, field, what=None):
+        def arrive(*args):
+            if what is not None:
+                receive_planes(what, *args)
+
+        def plane(dz, fresh):
+            @pl.loop(0, cells_x)
+            def _(i):
+                for j in range(cells_y):
+                    add_pairs(
+                        buffer, rule, i, j,
+                        [(dz, dx, k) for dx in inside(i) for k in range(3) if in_block(j, k)],
+                        fresh,
+                    )
+
+        every = (1, near, far)
+        plane(1, True)
+        for dz in (near, far):
+            arrive((dz,), 1, False)
+            plane(dz, False)
+        arrive(every, 1, True)
 
         @pl.loop(0, cells_x)
         def _(i):
-            for dx in outside(i):
-                for j in range(cells_y):
-                    for k in range(3):
-                        couple(i, j, 1, dx, k)
-            for dx in inside(i):
-                for j in range(cells_y):
-                    for k in range(3):
-                        if not in_block(j, k):
-                            couple(i, j, 1, dx, k)
-
-        receive(*opening, layers=(1, -1))
-
-        @pl.loop(0, cells_x)
-        def _(i):
-            @pl.loop(0, 6)
-            def _(plane):
-                dz, dx = 2 * (plane // 3), plane % 3
-                for j in range(cells_y):
-                    for k in range(3):
-                        couple(i, j, dz, dx, k)
-
-    def add_pairs(buffer, rule, i, j, total, planes, chosen):
-        for dz, dx in planes:
-            for k in range(3):
-                if not chosen(dz, dx, k):
-                    continue
-                tile = buffer.at[dz, i + dx]
-                block = pair[i * cells_y + j, (dz * 3 + dx) * 3 + k]
-                for s in range(2):
-                    at = row_at(s, j + k - 1, *rule)
-                    total[s] = total[s] + block * tile[at : at + 1, :]
-        return total
-
-    def operate_own(buffer, rule):
-        @pl.loop(0, cells_x)
-        def _(i):
+            for j in ends_y:
+                add_pairs(
+                    buffer, rule, i, j,
+                    [
+                        (dz, dx, k)
+                        for dz in every for dx in inside(i) for k in range(3)
+                        if not in_block(j, k)
+                    ],
+                    False,
+                )
+
+        @pl.loop(0, 2)
+        def _(turn):
+            side = jnp.where(turn == 0, early, 2 - early)
+            i = (cells_x - 1) * (side // 2)
+            arrive(every, side, False)
             for j in range(cells_y):
-                total = [jnp.zeros(shape, jnp.float32) for _ in range(2)]
-                total = add_pairs(
-                    buffer, rule, i, j, total,
-                    [(1, dx) for dx in inside(i)], lambda dz, dx, k: in_block(j, k),
+                add_pairs(
+                    buffer, rule, i, j,
+                    [(dz, side, k) for dz in every for k in range(3) if in_block(j, k)],
+                    False,
                 )
-                for s in range(2):
-                    sums[i, s * cells_y + j] = total[s]
-
-    def accumulate(buffer, rule, groups):
-        @pl.loop(0, cells_x)
-        def _(i):
-            for j in range(cells_y):
-                total = [sums[i, s * cells_y + j] for s in range(2)]
-                for planes, chosen in groups(i, j):
-                    total = add_pairs(buffer, rule, i, j, total, planes, chosen)
-                for s in range(2):
-                    sums[i, s * cells_y + j] = total[s]
-
-    even = lax.rem(me_z, 2) == 0
-    near = jnp.where(even, 2, 0)
-    far = 2 - near
-
-    def all_pairs(dz, dx, k):
-        return True
-
-    def operate_rest(buffer, rule, field, arrived=None):
-        if arrived is not None:
-            arrived(0)
-        accumulate(
-            buffer, rule,
-            lambda i, j: [
-                ([(1, dx) for dx in inside(i)], lambda dz, dx, k: not in_block(j, k)),
-                ([(1, dx) for dx in outside(i)], all_pairs),
-                ([(near, dx) for dx in range(3)], all_pairs),
-            ],
-        )
-        if arrived is not None:
-            arrived(1)
-        accumulate(
-            buffer, rule, lambda i, j: [([(far, dx) for dx in range(3)], all_pairs)]
-        )
-
-        out = []
-        for i in range(cells_x):
-            lines = []
-            for row in range(rows):
-                column = jnp.sum(sums[i, row], axis=1, keepdims=True)
-                lines.append(jnp.sum(jnp.where(eye, column, 0.0), axis=0, keepdims=True))
-            out.append(occ[i] * (stiff[i] * field[i] + jnp.concatenate(lines, axis=0)))
-        return out
+            arrive(every, side, True)
+            for j in ends_y:
+                add_pairs(
+                    buffer, rule, i, j,
+                    [(dz, side, k) for dz in every for k in range(3) if not in_block(j, k)],
+                    False,
+                )
+            gather(i)
+
+        return [occ[i] * (stiff[i] * field[i] + image[i]) for i in range(cells_x)]
 
     tile_shape = (rows, slots)
     lane = lax.broadcasted_iota(jnp.int32, tile_shape, 1)
@@ -376,25 +475,14 @@
         send(*what)
         if meanwhile is not None:
             meanwhile()
-        operate_own(buffer, field_rule)
-
-
-        def arrived(step):
-            for layer in (1, -1):
-                now = (near if step == 0 else far) == 1 - layer
-                pl.when(now)(lambda: receive(*what, layers=(layer,)))
-            if step == 0:
-                receive(*what, layers=(0,))
-
-        out = operate_rest(buffer, field_rule, field, arrived)
+        out = operate(buffer, field_rule, field, what)
         sent(*what)
         return out
 
-    build()
-    operate_own(first, start_rule)
-    image = operate_rest(first, start_rule, x)
+    build(opening)
+    started = operate(first, start_rule, x)
     sent(*opening)
-    r = [rhs[i] - image[i] for i in span]
+    r = [rhs[i] - started[i] for i in span]
     w = exchange_and_operate(1, r)
 
     p = s = z = None
@@ -438,15 +526,14 @@
     rows = 2 * cells_y
     devices = sizes[0] * sizes[1] * sizes[2]
     dys = (0, 1) if sizes[2] == 2 else (0, 1, -1)
-    messages = 9 * len(dys) - 1
     halo = (3, cells_x + 2)
     sides = len(dys) - 1
     vmem = pl.BlockSpec(memory_space=pltpu.VMEM)
     return pl.pallas_call(
         functools.partial(kernel, sizes, dys),
         out_shape=(
-            jax.ShapeDtypeStruct(type_ids.shape, jnp.float32),
-            jax.ShapeDtypeStruct((2,) + type_ids.shape, jnp.float32),
+            pltpu.VMEM(type_ids.shape, jnp.float32),
+            pltpu.VMEM((2,) + type_ids.shape, jnp.float32),
         ),
         in_specs=[pl.BlockSpec(memory_space=pl.ANY)] * 7,
         out_specs=(vmem, vmem),
@@ -458,13 +545,15 @@
             pltpu.VMEM((cells_x, 12, slots), jnp.float32),
             pltpu.VMEM((ITERS, cells_x, 4, slots), jnp.float32),
             pltpu.VMEM((cells, 27, slots, slots), jnp.float32),
-            pltpu.VMEM((cells, 4, slots, slots), jnp.float32),
+            pltpu.VMEM((cells, slots, DEPTH), jnp.bfloat16),
+            pltpu.VMEM((halo[0] * halo[1] * (cells_y + 2), DEPTH, 2 * slots), jnp.bfloat16),
             pltpu.VMEM((cells_x, rows, slots, slots), jnp.float32),
+            pltpu.VMEM((cells_x, rows, slots), jnp.float32),
             pltpu.VMEM((ITERS, devices - 1, 1, slots), jnp.float32),
             pltpu.VMEM((ITERS, 1, slots), jnp.float32),
             pltpu.SemaphoreType.DMA((len(arrays),)),
-            pltpu.SemaphoreType.DMA((ITERS + 1, messages)),
-            pltpu.SemaphoreType.DMA((ITERS + 1, messages)),
+            pltpu.SemaphoreType.DMA((ITERS + 1, 3, 3, len(dys))),
+            pltpu.SemaphoreType.DMA((ITERS + 1, 3, 3, len(dys))),
             pltpu.SemaphoreType.DMA((ITERS,)),
             pltpu.SemaphoreType.DMA((ITERS,)),
         ],

time: 57.6 us -> 45.4 us (0.79)
  Pallas kernels: 54.9 us -> 43.4 us
  local copies, waits for them, and re-layouts: 1.88 us -> 1.19 us
    pallas_call x1, Pallas kernels: 54.9 us -> 43.4 us  [per_device(): pl.pallas_call(functools.partial(kernel, sizes, dys), out_shape=(pltpu.VM...]
    unnamed x4 -> x2, local copies, waits for them, and re-layouts: 1.88 us -> 1.19 us
where the time goes in v1:
time: 45.4 us; the launch traced here: 45.2 us
  Pallas kernels  43.4 us (96%)
  local copies, waits for them, and re-layouts  1.19 us (3%)
  between operations  0.64 us (1%)
    pallas_call x1, Pallas kernels, per_device(): pl.pallas_call(functools.partial(kernel, sizes, dys), out_shape=(pltpu.VM...  43.4 us
    unnamed x2, local copies, waits for them, and re-layouts  1.19 us

profile of v1, /device:TPU:0, one launch (start us, length us, event | category | flops | bytes accessed | tf_op | source)
XLA Modules:
  0.0 45.2 jit_solution(3227291458465863573)
XLA Ops:
  0.6 43.4 %shard_map.86 = (f32[1,2,4,128]{3,2,1,0:T(4,128)S(1)}, f32[2,1,2,4,128]{4,3,2,1,0:T(4,128)S(1)}) custom-call(f32[3,1,2,4,128]{4,3,2,1,0:T(4,128)} %offsets_in.1, s32[1,2,4,128]{3,2,1,0:T(4,128)} %type_ids_in.1, s32[1,2,4,128]{3,2,1,0:T(4,128)} %occupied_in.1, f32[2,1,2,4,128]{4,3,2,1,0:T(4,128)} %prior_in.1, f32[3]{0:T(128)} %electro_in.1, f32[3]{0:T(128)} %hardness_in.1, ...), custom_call_target="tpu_custom_call" | custom-call | tf_op jit(solution)/shard_map/pallas_call | solution.py:532
  44.0 0.6 %copy.11 = f32[1,2,4,128]{3,2,1,0:T(4,128)} copy(f32[1,2,4,128]{3,2,1,0:T(4,128)S(1)} %get-tuple-element.2) | data formatting | bytes 8192
  44.6 0.6 %copy.12 = f32[2,1,2,4,128]{4,3,2,1,0:T(4,128)} copy(f32[2,1,2,4,128]{4,3,2,1,0:T(4,128)S(1)} %get-tuple-element.3) | data formatting | bytes 16384

commit v2 on v1

--- a/solution.py
+++ b/solution.py
@@ -274,9 +274,9 @@
         for part in range(slots // CHUNK):
             span = pl.ds(part * CHUNK, CHUNK)
             both = jnp.dot(left[cell, span], other, preferred_element_type=jnp.float32)
-            squared = jnp.maximum(both[:, :slots], 1e-30)
+            squared = jnp.clip(both[:, :slots], 1e-30, EDGE * EDGE)
             apart = squared * lax.rsqrt(squared)
-            reach = jnp.maximum(EDGE - apart, 0.0)
+            reach = EDGE - apart
             reach = reach * reach
             pair[cell, (dz * 3 + dx) * 3 + k, span] = (
                 reach * reach * (apart + EDGE / 4) * lax.rsqrt(both[:, slots:])
@@ -284,15 +284,17 @@
 
     ends_y = sorted({0, cells_y - 1})
 
+    every = (1, near, far)
+    inner, outer = range(cells_y), (-1, cells_y)
+
     def build(what):
         def plane(dz):
             @pl.loop(0, cells_x)
             def _(i):
-                for y in range(cells_y):
+                for y in inner:
                     offer(dz, i + 1, y)
 
-            @pl.loop(0, cells_x)
-            def _(i):
+            for i in range(cells_x):
                 for j in range(cells_y):
                     for dx in inside(i):
                         for k in range(3):
@@ -308,45 +310,38 @@
         for dz in (near, far):
             receive_planes(what, (dz,), 1, False)
             plane(dz)
-        receive_planes(what, (1, near, far), 1, True)
-        for dz in (1, near, far):
+        receive_planes(what, every, 1, True)
+        for dz in every:
 
             @pl.loop(0, cells_x)
             def _(i):
-                for y in (-1, cells_y):
+                for y in outer:
                     offer(dz, i + 1, y)
 
-        @pl.loop(0, cells_x)
-        def _(i):
-            for dz in (1, near, far):
+        for i in range(cells_x):
+            for dz in every:
                 for j in ends_y:
                     for dx in inside(i):
                         for k in range(3):
                             if not in_block(j, k):
                                 couple(i, j, dz, dx, k)
 
-        @pl.loop(0, 2)
-        def _(turn):
-            side = jnp.where(turn == 0, early, 2 - early)
-            i = (cells_x - 1) * (side // 2)
-            receive_planes(what, (1, near, far), side, False)
-            for dz in (1, near, far):
-                for y in range(cells_y):
-                    offer(dz, i + side, y)
-            for dz in (1, near, far):
-                for j in range(cells_y):
-                    for k in range(3):
-                        if in_block(j, k):
-                            couple(i, j, dz, side, k)
-            receive_planes(what, (1, near, far), side, True)
-            for dz in (1, near, far):
-                for y in (-1, cells_y):
-                    offer(dz, i + side, y)
-            for dz in (1, near, far):
-                for j in ends_y:
-                    for k in range(3):
-                        if not in_block(j, k):
-                            couple(i, j, dz, side, k)
+    def side_of(turn):
+        side = early if turn == 0 else 2 - early
+        return side, (cells_x - 1) * (side // 2)
+
+    def accept(what, side, i):
+        receive_planes(what, every, side, False)
+        receive_planes(what, every, side, True)
+        for dz in every:
+            for y in (*inner, *outer):
+                offer(dz, i + side, y)
+
+    def couple_side(side, i):
+        for dz in every:
+            for j in range(cells_y):
+                for k in range(3):
+                    couple(i, j, dz, side, k)
 
     def add_pairs(buffer, rule, i, j, entries, fresh):
         if fresh:
@@ -369,62 +364,73 @@
             lines.append(jnp.sum(jnp.where(eye, column, 0.0), axis=0, keepdims=True))
         image[i] = jnp.concatenate(lines, axis=0)
 
-    def operate(buffer, rule, field, what=None):
-        def arrive(*args):
-            if what is not None:
-                receive_planes(what, *args)
-
+    def update(field):
+        return [occ[i] * (stiff[i] * field[i] + image[i]) for i in range(cells_x)]
+
+    def plane_pairs(dz, i, j):
+        return [(dz, dx, k) for dx in inside(i) for k in range(3) if in_block(j, k)]
+
+    def end_pairs(i, j):
+        return [
+            (dz, dx, k)
+            for dz in every for dx in inside(i) for k in range(3)
+            if not in_block(j, k)
+        ]
+
+    def first_image(what, field):
+        buffer, rule = what[1], start_rule
+
+        @pl.loop(0, cells_x)
+        def _(i):
+            for j in range(cells_y):
+                pairs = [p for dz in every for p in plane_pairs(dz, i, j)] + end_pairs(i, j)
+                add_pairs(buffer, rule, i, j, pairs, True)
+
+        sides = [side_of(turn) for turn in range(2)]
+        for side, i in sides:
+            accept(what, side, i)
+            couple_side(side, i)
+
+        @pl.loop(0, cells_x)
+        def _(i):
+            side = 2 * i
+            for j in range(cells_y):
+                pairs = [(dz, side, k) for dz in every for k in range(3)]
+                add_pairs(buffer, rule, i, j, pairs, False)
+            gather(i)
+
+        return update(field)
+
+    def operate(buffer, rule, field, what):
         def plane(dz, fresh):
             @pl.loop(0, cells_x)
             def _(i):
                 for j in range(cells_y):
-                    add_pairs(
-                        buffer, rule, i, j,
-                        [(dz, dx, k) for dx in inside(i) for k in range(3) if in_block(j, k)],
-                        fresh,
-                    )
-
-        every = (1, near, far)
+                    add_pairs(buffer, rule, i, j, plane_pairs(dz, i, j), fresh)
+
         plane(1, True)
         for dz in (near, far):
-            arrive((dz,), 1, False)
+            receive_planes(what, (dz,), 1, False)
             plane(dz, False)
-        arrive(every, 1, True)
+        receive_planes(what, every, 1, True)
 
         @pl.loop(0, cells_x)
         def _(i):
             for j in ends_y:
-                add_pairs(
-                    buffer, rule, i, j,
-                    [
-                        (dz, dx, k)
-                        for dz in every for dx in inside(i) for k in range(3)
-                        if not in_block(j, k)
-                    ],
-                    False,
-                )
+                add_pairs(buffer, rule, i, j, end_pairs(i, j), False)
 
         @pl.loop(0, 2)
         def _(turn):
             side = jnp.where(turn == 0, early, 2 - early)
             i = (cells_x - 1) * (side // 2)
-            arrive(every, side, False)
-            for j in range(cells_y):
-                add_pairs(
-                    buffer, rule, i, j,
-                    [(dz, side, k) for dz in every for k in range(3) if in_block(j, k)],
-                    False,
-                )
-            arrive(every, side, True)
-            for j in ends_y:
-                add_pairs(
-                    buffer, rule, i, j,
-                    [(dz, side, k) for dz in every for k in range(3) if not in_block(j, k)],
-                    False,
-                )
+            for within in (True, False):
+                receive_planes(what, every, side, not within)
+                for j in range(cells_y) if within else ends_y:
+                    pairs = [(dz, side, k) for dz in every for k in range(3) if in_block(j, k) == within]
+                    add_pairs(buffer, rule, i, j, pairs, False)
             gather(i)
 
-        return [occ[i] * (stiff[i] * field[i] + image[i]) for i in range(cells_x)]
+        return update(field)
 
     tile_shape = (rows, slots)
     lane = lax.broadcasted_iota(jnp.int32, tile_shape, 1)
@@ -480,7 +486,7 @@
         return out
 
     build(opening)
-    started = operate(first, start_rule, x)
+    started = first_image(opening, x)
     sent(*opening)
     r = [rhs[i] - started[i] for i in span]
     w = exchange_and_operate(1, r)

time: 45.4 us -> 44 us (0.969)
  Pallas kernels: 43.4 us -> 42 us
    pallas_call x1, Pallas kernels: 43.4 us -> 42 us  [per_device(): pl.pallas_call(functools.partial(kernel, sizes, dys), out_shape=(pltpu.VM...]
where the time goes in v2:
time: 44 us; the launch traced here: 43.8 us
  Pallas kernels  42 us (95%)
  local copies, waits for them, and re-layouts  1.19 us (3%)
  between operations  0.64 us (1%)
    pallas_call x1, Pallas kernels, per_device(): pl.pallas_call(functools.partial(kernel, sizes, dys), out_shape=(pltpu.VM...  42 us
    unnamed x2, local copies, waits for them, and re-layouts  1.19 us

profile of v2, /device:TPU:0, one launch (start us, length us, event | category | flops | bytes accessed | tf_op | source)
XLA Modules:
  0.0 43.8 jit_solution(16210890367589015142)
XLA Ops:
  0.6 42.0 %shard_map.86 = (f32[1,2,4,128]{3,2,1,0:T(4,128)S(1)}, f32[2,1,2,4,128]{4,3,2,1,0:T(4,128)S(1)}) custom-call(f32[3,1,2,4,128]{4,3,2,1,0:T(4,128)} %offsets_in.1, s32[1,2,4,128]{3,2,1,0:T(4,128)} %type_ids_in.1, s32[1,2,4,128]{3,2,1,0:T(4,128)} %occupied_in.1, f32[2,1,2,4,128]{4,3,2,1,0:T(4,128)} %prior_in.1, f32[3]{0:T(128)} %electro_in.1, f32[3]{0:T(128)} %hardness_in.1, ...), custom_call_target="tpu_custom_call" | custom-call | tf_op jit(solution)/shard_map/pallas_call | solution.py:538
  42.6 0.6 %copy.11 = f32[1,2,4,128]{3,2,1,0:T(4,128)} copy(f32[1,2,4,128]{3,2,1,0:T(4,128)S(1)} %get-tuple-element.2) | data formatting | bytes 8192
  43.2 0.6 %copy.12 = f32[2,1,2,4,128]{4,3,2,1,0:T(4,128)} copy(f32[2,1,2,4,128]{4,3,2,1,0:T(4,128)S(1)} %get-tuple-element.3) | data formatting | bytes 16384

commit v3 on v2

--- a/solution.py
+++ b/solution.py
@@ -284,40 +284,49 @@
 
     ends_y = sorted({0, cells_y - 1})
 
-    every = (1, near, far)
+    own = 1
+    every = (own, near, far)
     inner, outer = range(cells_y), (-1, cells_y)
 
     def build(what):
         def plane(dz):
-            @pl.loop(0, cells_x)
-            def _(i):
+            mirrored = []
+            for i in range(cells_x):
                 for y in inner:
                     offer(dz, i + 1, y)
-
             for i in range(cells_x):
                 for j in range(cells_y):
                     for dx in inside(i):
                         for k in range(3):
-                            if in_block(j, k):
+                            if not in_block(j, k):
+                                continue
+                            if dz is not own or (dx, k) >= (1, 1):
                                 couple(i, j, dz, dx, k)
+                            else:
+                                mirrored.append((i, j, dx, k))
+            for i, j, dx, k in mirrored:
+                there = (i + dx - 1) * cells_y + j + k - 1
+                values = pair[there, (3 + 2 - dx) * 3 + 2 - k]
+                pair[i * cells_y + j, (3 + dx) * 3 + k] = values.T
+
+        for i in range(cells_x):
+            for j in range(cells_y):
+                take(i, j)
+        plane(own)
 
         @pl.loop(0, cells_x)
         def _(i):
             for j in range(cells_y):
-                take(i, j)
-
-        plane(1)
+                add_pairs(what[1], start_rule, i, j, plane_pairs(own, i, j), True)
+
         for dz in (near, far):
             receive_planes(what, (dz,), 1, False)
             plane(dz)
         receive_planes(what, every, 1, True)
         for dz in every:
-
-            @pl.loop(0, cells_x)
-            def _(i):
+            for i in range(cells_x):
                 for y in outer:
                     offer(dz, i + 1, y)
-
         for i in range(cells_x):
             for dz in every:
                 for j in ends_y:
@@ -383,8 +392,8 @@
         @pl.loop(0, cells_x)
         def _(i):
             for j in range(cells_y):
-                pairs = [p for dz in every for p in plane_pairs(dz, i, j)] + end_pairs(i, j)
-                add_pairs(buffer, rule, i, j, pairs, True)
+                pairs = plane_pairs(near, i, j) + plane_pairs(far, i, j) + end_pairs(i, j)
+                add_pairs(buffer, rule, i, j, pairs, False)
 
         sides = [side_of(turn) for turn in range(2)]
         for side, i in sides:

time: 44 us -> 43.3 us (0.984)
  Pallas kernels: 42 us -> 41.3 us
    pallas_call x1, Pallas kernels: 42 us -> 41.3 us  [per_device(): pl.pallas_call(functools.partial(kernel, sizes, dys), out_shape=(pltpu.VM...]
where the time goes in v3:
time: 43.3 us; the launch traced here: 43.1 us
  Pallas kernels  41.3 us (95%)
  local copies, waits for them, and re-layouts  1.19 us (3%)
  between operations  0.64 us (1%)
    pallas_call x1, Pallas kernels, per_device(): pl.pallas_call(functools.partial(kernel, sizes, dys), out_shape=(pltpu.VM...  41.3 us
    unnamed x2, local copies, waits for them, and re-layouts  1.19 us

profile of v3, /device:TPU:0, one launch (start us, length us, event | category | flops | bytes accessed | tf_op | source)
XLA Modules:
  0.0 43.1 jit_solution(16784191277519354041)
XLA Ops:
  0.6 41.3 %shard_map.86 = (f32[1,2,4,128]{3,2,1,0:T(4,128)S(1)}, f32[2,1,2,4,128]{4,3,2,1,0:T(4,128)S(1)}) custom-call(f32[3,1,2,4,128]{4,3,2,1,0:T(4,128)} %offsets_in.1, s32[1,2,4,128]{3,2,1,0:T(4,128)} %type_ids_in.1, s32[1,2,4,128]{3,2,1,0:T(4,128)} %occupied_in.1, f32[2,1,2,4,128]{4,3,2,1,0:T(4,128)} %prior_in.1, f32[3]{0:T(128)} %electro_in.1, f32[3]{0:T(128)} %hardness_in.1, ...), custom_call_target="tpu_custom_call" | custom-call | tf_op jit(solution)/shard_map/pallas_call | solution.py:547
  41.9 0.6 %copy.11 = f32[1,2,4,128]{3,2,1,0:T(4,128)} copy(f32[1,2,4,128]{3,2,1,0:T(4,128)S(1)} %get-tuple-element.2) | data formatting | bytes 8192
  42.5 0.6 %copy.12 = f32[2,1,2,4,128]{4,3,2,1,0:T(4,128)} copy(f32[2,1,2,4,128]{4,3,2,1,0:T(4,128)S(1)} %get-tuple-element.3) | data formatting | bytes 16384

commit v4 on v3

--- a/solution.py
+++ b/solution.py
@@ -16,7 +16,7 @@
 CHUNK = 64
 EDGE = (4.0 * coulomb_factor / cell_edge) ** 0.25
 SCALE = EDGE / cell_edge
-DEPTH = 64
+DEPTH = 32
 
 
 def kernel(
@@ -54,17 +54,17 @@
     def each_peer(action):
         def layer(dz, skip):
             z = lax.rem(me_z + dz, nz)
-            for dx in range(nx):
-                for dy in range(ny):
+            for dx in (*range(1, nx, 2), *range(2, nx, 2), 0):
+                for dy in reversed(range(ny)):
                     if not (skip and dx == 0 and dy == 0):
                         action((z, at_x[dx], at_y[dy]), (dz * nx + dx) * ny + dy - 1)
 
-        layer(0, True)
         if nz <= 4:
             for dz in range(1, nz):
                 layer(dz, False)
         else:
             pl.loop(1, nz)(lambda dz: layer(dz, False))
+        layer(0, True)
 
     barrier = pltpu.get_barrier_semaphore()
     each_peer(
@@ -211,8 +211,6 @@
     group = lax.broadcasted_iota(jnp.int32, (8, slots), 0)
     role = lax.rem(group, 4)
     lower = group < 4
-    ones = jnp.where(group < 3, 1.0, 0.0)
-    nought = jnp.zeros((8, slots), jnp.float32)
 
     def split(values):
         pieces = []
@@ -241,15 +239,17 @@
 
     def offer(dz, dx, y):
         moved, length, spread = place(dz, dx, y)
-        last = jnp.where(lower, length, length + spread)
-        p1, p2, p3 = split(jnp.where(role == 3, last, moved))
+        p1, p2, p3 = split(jnp.where(role == 3, length, moved))
+        s1, s2, s3 = split(spread)
+        shared = [jnp.where(lower, p1, p2), jnp.where(lower, p3, p1)]
+        third = jnp.where(lower, p2, p1)
+        ends_of = [
+            (0.0, jnp.where(group < 3, 1.0, 0.0)),
+            (s3, jnp.where(group < 3, 0.0, jnp.where(group < 6, 1.0, jnp.where(group == 6, s1, s2)))),
+        ]
         to = slot_at(dz, dx, y)
-        for half in range(2):
-            kept = [
-                jnp.where(lower, p, 0.0) if half == 0 else jnp.where(lower, 0.0, p)
-                for p in (p1, p2, p3)
-            ]
-            lines = [kept[q] for q in (0, 1, 2, 0, 1, 0)] + [ones, ones if half else nought]
+        for half, (spare, fourth) in enumerate(ends_of):
+            lines = shared + [jnp.where(group == 3, spare, third), fourth]
             right[to, :, half * slots : (half + 1) * slots] = jnp.concatenate(
                 lines, axis=0
             ).astype(jnp.bfloat16)
@@ -257,15 +257,16 @@
     def take(i, j):
         moved, length, spread = place(1, i + 1, j)
         a1, a2, a3 = split(-2.0 * moved)
-
-        def stacked(value):
-            v1, v2, v3 = split(value)
-            return jnp.where(group == 0, v1, jnp.where(group == 1, v2, jnp.where(group == 2, v3, 0.0)))
-
-        one = jnp.where(role == 3, 1.0, a1)
-        two = jnp.where(role == 3, 0.0, a2)
-        three = jnp.where(role == 3, 0.0, a3)
-        lines = [one, one, one, two, two, three, stacked(length), stacked(spread)]
+        fourth = jnp.ones((8, slots), jnp.float32)
+        for at, piece in enumerate(split(length) + split(length + spread)):
+            fourth = jnp.where(group == at, piece, fourth)
+        last = role == 3
+        lines = [
+            jnp.where(last, 1.0, a1),
+            jnp.where(lower, jnp.where(last, 1.0, a1), jnp.where(last, 0.0, a2)),
+            jnp.where(lower, jnp.where(last, 1.0, a2), jnp.where(last, 0.0, a3)),
+            fourth,
+        ]
         left[i * cells_y + j] = jnp.concatenate(lines, axis=0).T.astype(jnp.bfloat16)
 
     def couple(i, j, dz, dx, k):

time: 43.3 us -> 43 us (level)
  no operation moved by 1% of the time
where the time goes in v4:
time: 43 us; the launch traced here: 42.8 us
  Pallas kernels  40.9 us (95%)
  local copies, waits for them, and re-layouts  1.19 us (3%)
  between operations  0.64 us (1%)
    pallas_call x1, Pallas kernels, per_device(): pl.pallas_call(functools.partial(kernel, sizes, dys), out_shape=(pltpu.VM...  40.9 us
    unnamed x2, local copies, waits for them, and re-layouts  1.19 us

profile of v4, /device:TPU:0, one launch (start us, length us, event | category | flops | bytes accessed | tf_op | source)
XLA Modules:
  0.0 42.8 jit_solution(3594737587775596593)
XLA Ops:
  0.6 40.9 %shard_map.86 = (f32[1,2,4,128]{3,2,1,0:T(4,128)S(1)}, f32[2,1,2,4,128]{4,3,2,1,0:T(4,128)S(1)}) custom-call(f32[3,1,2,4,128]{4,3,2,1,0:T(4,128)} %offsets_in.1, s32[1,2,4,128]{3,2,1,0:T(4,128)} %type_ids_in.1, s32[1,2,4,128]{3,2,1,0:T(4,128)} %occupied_in.1, f32[2,1,2,4,128]{4,3,2,1,0:T(4,128)} %prior_in.1, f32[3]{0:T(128)} %electro_in.1, f32[3]{0:T(128)} %hardness_in.1, ...), custom_call_target="tpu_custom_call" | custom-call | tf_op jit(solution)/shard_map/pallas_call | solution.py:548
  41.6 0.6 %copy.11 = f32[1,2,4,128]{3,2,1,0:T(4,128)} copy(f32[1,2,4,128]{3,2,1,0:T(4,128)S(1)} %get-tuple-element.2) | data formatting | bytes 8192
  42.2 0.6 %copy.12 = f32[2,1,2,4,128]{4,3,2,1,0:T(4,128)} copy(f32[2,1,2,4,128]{4,3,2,1,0:T(4,128)S(1)} %get-tuple-element.3) | data formatting | bytes 16384
